TPU v7x, 32 devices: a whole 2x2x4 slice. The times are simulated.
32 devices in a mesh: row: 2 (over x), col: 16 (over z, y, core).
Axes of the slice: x: 2, y: 2, z: 4, core: 2. Of those that a mesh axis runs over, the one named last changes fastest.
Arguments:
- tokens: bfloat16 [512, 4608], P('col', 'row'), may hold values from -6 to 6
- pre_gain: float32 [2, 4608], P(None, 'row'), may hold values from -0.6 to 0.6
- post_gain: float32 [2, 4608], P(None, 'row'), may hold values from -0.6 to 0.6
- gate_weight: bfloat16 [2, 4608, 36864], P(None, ('row', 'col')), may hold values from -0.09375 to 0.09375
- up_weight: bfloat16 [2, 4608, 36864], P(None, ('row', 'col')), may hold values from -0.09375 to 0.09375
- down_weight: bfloat16 [2, 36864, 4608], P(None, ('row', 'col')), may hold values from -0.13541667 to 0.13541667
Outputs:
- stream: bfloat16 [512, 4608], P('col', 'row')
All inputs are finite; a program needn't handle non-finite values.
Results may differ from a plain program's by a relative error of at most 0.019.
Values may be sent and summed in bfloat16 or wider, within the bound.
A program may use at most 256 MiB of HBM per device.

v0:
```python
import jax
import jax.numpy as jnp
from jax import lax
from jax.sharding import PartitionSpec as P

norm_eps = 1e-06


def activate(summed, columns):
    gate = summed[:, :columns]
    up_proj = summed[:, columns:]
    return (jax.nn.gelu(gate, approximate=True) * up_proj).astype(jnp.bfloat16)


def on_device(tokens, pre_gain, post_gain, gate_weight, up_weight, down_weight):
    layer_count = gate_weight.shape[0]
    row_count = lax.axis_size("row")
    col_count = lax.axis_size("col")
    model_width = tokens.shape[1] * row_count
    stored_rows = gate_weight.shape[1]
    hidden_total = gate_weight.shape[2]
    block_width = hidden_total // (row_count * col_count)
    tile_rows = stored_rows * col_count
    tile_columns = hidden_total // col_count
    current = tokens
    for layer_index in range(layer_count):
        gate_split = gate_weight[layer_index].reshape(
            stored_rows, row_count, col_count, block_width
        )
        up_split = up_weight[layer_index].reshape(stored_rows, row_count, col_count, block_width)
        gate_tile, up_tile = (
            lax.all_to_all(gate_split, "col", split_axis=2, concat_axis=0, tiled=True),
            lax.all_to_all(up_split, "col", split_axis=2, concat_axis=0, tiled=True),
        )
        gate_up = jnp.concatenate(
            (gate_tile.reshape(tile_rows, tile_columns), up_tile.reshape(tile_rows, tile_columns)),
            axis=1,
        )
        down_tile = lax.all_to_all(
            down_weight[layer_index], "row", split_axis=1, concat_axis=0, tiled=True
        )
        columns = gate_up.shape[1] // 2
        values = current.astype(jnp.float32)
        squares = lax.psum(jnp.sum(values * values, axis=1), "row")
        scale_pre = lax.rsqrt(squares / model_width + norm_eps)[:, None]
        normed = (values * scale_pre * (1.0 + pre_gain[layer_index])[None, :]).astype(jnp.bfloat16)
        partial_sums = jnp.dot(
            lax.all_gather(normed, "col", axis=0, tiled=True),
            gate_up,
            preferred_element_type=jnp.float32,
        )
        summed = lax.psum(partial_sums.astype(jnp.bfloat16), "row").astype(jnp.float32)
        hidden = activate(summed, columns)
        branch = lax.psum_scatter(
            jnp.dot(hidden, down_tile, preferred_element_type=jnp.float32),
            "col",
            scatter_dimension=0,
            tiled=True,
        )
        branch_squares = lax.psum(jnp.sum(branch * branch, axis=1), "row")
        scale_post = lax.rsqrt(branch_squares / model_width + norm_eps)[:, None]
        post = branch * scale_post * (1.0 + post_gain[layer_index])[None, :]
        current = (values + post).astype(jnp.bfloat16)
    return current


def solution(mesh):
    in_specs = (
        P("col", "row"),
        P(None, "row"),
        P(None, "row"),
        P(None, ("row", "col"), None),
        P(None, ("row", "col"), None),
        P(None, ("row", "col"), None),
    )
    out_specs = P("col", "row")
    return jax.shard_map(
        on_device, mesh=mesh, in_specs=in_specs, out_specs=out_specs, check_vma=False
    )
```

profile of v0, /device:TPU:0, one launch (start us, length us, event | category | flops | bytes accessed | tf_op | source)
XLA Modules:
  0.0 1513.6 jit_solution(6877893643753962465)
XLA Ops:
  6.5 15.8 %fusion.65 = (bf16[1,1152,4608]{2,1,0:T(8,128)(2,1)}, bf16[1,1152,4608]{2,1,0:T(8,128)(2,1)}) fusion(bf16[2,1152,4608]{2,1,0:T(8,128)(2,1)} %param.11), kind=kLoop, calls=%fused_computation.76 | loop fusion | bytes 42467328 | tf_op jit(solution)/shard_map/slice | solution.py:40
  22.3 15.2 %copy.19 = bf16[1,1152,4608]{1,2,0:T(8,128)(2,1)} copy(bf16[1,1152,4608]{2,1,0:T(8,128)(2,1)} %get-tuple-element.16) | data formatting | bytes 21233664
  45.4 12.6 fusion.63
  61.7 15.8 %copy.11 = bf16[144,2,16,1152]{3,1,0,2:T(2,128)(2,1)} copy(bf16[144,2,16,1152]{3,2,1,0:T(8,128)(2,1)S(1)} %bitcast.56) | data formatting | bytes 21233664 | tf_op jit(solution)/shard_map/reshape;squeeze | solution.py:27
  77.5 85.5 %all-to-all-done.2 = bf16[1152,2,2304]{0,2,1:T(8,128)(2,1)} async-done(((bf16[1152,2,2304]{0,2,1:T(8,128)(2,1)}), bf16[1152,2,2304]{0,2,1:T(8,128)(2,1)}, u32[]{:S(2)}, u32[]{:S(2)}) %all-to-all-start.2) | async-done | bytes 10616864 | tf_op jit(solution)/shard_map/all_to_all | solution.py:39
  169.3 12.6 fusion.64
  185.5 15.8 %copy.12 = bf16[144,2,16,1152]{3,1,0,2:T(2,128)(2,1)} copy(bf16[144,2,16,1152]{3,2,1,0:T(8,128)(2,1)S(1)} %bitcast.57) | data formatting | bytes 21233664 | tf_op jit(solution)/shard_map/reshape;squeeze | solution.py:30
  201.4 157.3 %all-to-all-done = bf16[144,2,16,1152]{3,1,0,2:T(2,128)(2,1)} async-done(((bf16[144,2,16,1152]{3,1,0,2:T(2,128)(2,1)}), bf16[144,2,16,1152]{3,1,0,2:T(2,128)(2,1)}, u32[]{:S(2)}, u32[]{:S(2)}) %all-to-all-start) | async-done | bytes 10616864 | tf_op jit(solution)/shard_map/all_to_all | solution.py:32
  358.7 45.5 %all-to-all-start.1 = ((bf16[144,2,16,1152]{3,1,0,2:T(2,128)(2,1)}), bf16[144,2,16,1152]{3,1,0,2:T(2,128)(2,1)}, u32[]{:S(2)}, u32[]{:S(2)}) async-start(bf16[144,2,16,1152]{3,1,0,2:T(2,128)(2,1)} %copy.12), calls=%async_computation.1 | async-start | bytes 21233664 | tf_op jit(solution)/shard_map/all_to_all | solution.py:33
  411.3 15.8 %copy.15 = bf16[144,2,16,1152]{3,1,0,2:T(2,128)(2,1)} copy(bf16[144,2,16,1152]{3,2,1,0:T(8,128)(2,1)S(1)} %bitcast.58) | data formatting | bytes 21233664 | tf_op jit(solution)/shard_map/reshape;squeeze | solution.py:27
  427.2 166.4 %all-to-all-done.1 = bf16[144,2,16,1152]{3,1,0,2:T(2,128)(2,1)} async-done(((bf16[144,2,16,1152]{3,1,0,2:T(2,128)(2,1)}), bf16[144,2,16,1152]{3,1,0,2:T(2,128)(2,1)}, u32[]{:S(2)}, u32[]{:S(2)}) %all-to-all-start.1) | async-done | bytes 10616864 | tf_op jit(solution)/shard_map/all_to_all | solution.py:33
  593.6 45.5 %all-to-all-start.3 = ((bf16[144,2,16,1152]{3,1,0,2:T(2,128)(2,1)}), bf16[144,2,16,1152]{3,1,0,2:T(2,128)(2,1)}, u32[]{:S(2)}, u32[]{:S(2)}) async-start(bf16[144,2,16,1152]{3,1,0,2:T(2,128)(2,1)} %copy.15), calls=%async_computation.4 | async-start | bytes 21233664 | tf_op jit(solution)/shard_map/all_to_all | solution.py:32
  652.2 15.9 %copy.16 = bf16[144,2,16,1152]{3,1,0,2:T(2,128)(2,1)} copy(bf16[144,2,16,1152]{3,2,1,0:T(8,128)(2,1)S(1)} %bitcast.59) | data formatting | bytes 21233664 | tf_op jit(solution)/shard_map/reshape;squeeze | solution.py:30
  668.1 11.3 copy.22
  679.4 11.3 copy.24
  690.7 152.0 %all-to-all-done.3 = bf16[144,2,16,1152]{3,1,0,2:T(2,128)(2,1)} async-done(((bf16[144,2,16,1152]{3,1,0,2:T(2,128)(2,1)}), bf16[144,2,16,1152]{3,1,0,2:T(2,128)(2,1)}, u32[]{:S(2)}, u32[]{:S(2)}) %all-to-all-start.3) | async-done | bytes 10616864 | tf_op jit(solution)/shard_map/all_to_all | solution.py:32
  842.7 45.4 %all-to-all-start.4 = ((bf16[144,2,16,1152]{3,1,0,2:T(2,128)(2,1)}), bf16[144,2,16,1152]{3,1,0,2:T(2,128)(2,1)}, u32[]{:S(2)}, u32[]{:S(2)}) async-start(bf16[144,2,16,1152]{3,1,0,2:T(2,128)(2,1)} %copy.16), calls=%async_computation.5 | async-start | bytes 21233664 | tf_op jit(solution)/shard_map/all_to_all | solution.py:33
  888.4 16.6 %fusion.11 = bf16[512,4608]{1,0:T(8,128)(2,1)} fusion(bf16[512,2304]{1,0:T(8,128)(2,1)} %all-gather.3.cloned.1.call-done, bf16[2304,2304]{1,0:T(8,128)(2,1)} %bitcast.66, bf16[2304,2304]{1,0:T(8,128)(2,1)} %bitcast.64), kind=kOutput, calls=%fused_computation.9 | convolution fusion | flops 10916462592 | bytes 28311552 | tf_op jit(solution)/shard_map/dot_general | solution.py:47
  905.1 15.6 %copy.14 = bf16[2,1152,2304]{2,1,0:T(8,128)(2,1)} copy(bf16[2,1152,2304]{1,2,0:T(8,128)(2,1)} %bitcast.5) | data formatting | bytes 21233664 | tf_op jit(solution)/shard_map/all_to_all | solution.py:39
  920.7 104.1 %all-reduce.3.cloned.1.call-done = bf16[512,4608]{1,0:T(8,128)(2,1)} async-done(((bf16[512,4608]{1,0:T(8,128)(2,1)}), bf16[512,4608]{1,0:T(8,128)(2,1)}) %all-reduce.3.cloned.1.call-update) | async-done | bytes 4718608 | tf_op jit(solution)/shard_map/psum | solution.py:52
  1030.2 8.3 fusion.34
  1038.7 93.3 %reduce-scatter.3.cloned.1.call-done = f32[32,2304]{1,0:T(8,128)} async-done(((f32[512,2304]{1,0:T(8,128)}), f32[32,2304]{1,0:T(8,128)}) %reduce-scatter.3.cloned.1.call-update) | async-done | bytes 294928 | tf_op jit(solution)/shard_map/reduce_scatter | solution.py:54
  1145.0 15.3 %copy.20 = bf16[1,1152,4608]{1,2,0:T(8,128)(2,1)} copy(bf16[1,1152,4608]{2,1,0:T(8,128)(2,1)} %get-tuple-element.15) | data formatting | bytes 21233664
  1160.2 11.4 copy.26
  1179.6 11.4 copy.28
  1191.0 11.0 all-gather.5.cloned.1.call-done
  1202.0 16.7 %fusion.8 = bf16[512,4608]{1,0:T(8,128)(2,1)} fusion(bf16[512,2304]{1,0:T(8,128)(2,1)} %all-gather.5.cloned.1.call-done, bf16[2304,2304]{1,0:T(8,128)(2,1)} %bitcast.68, bf16[2304,2304]{1,0:T(8,128)(2,1)} %bitcast.65), kind=kOutput, calls=%fused_computation.8 | convolution fusion | flops 10916462592 | bytes 28311552 | tf_op jit(solution)/shard_map/dot_general | solution.py:47
  1218.7 128.1 %all-to-all-done.5 = bf16[1152,2,2304]{0,2,1:T(8,128)(2,1)} async-done(((bf16[1152,2,2304]{0,2,1:T(8,128)(2,1)}), bf16[1152,2,2304]{0,2,1:T(8,128)(2,1)}, u32[]{:S(2)}, u32[]{:S(2)}) %all-to-all-start.5) | async-done | bytes 10616864 | tf_op jit(solution)/shard_map/all_to_all | solution.py:39
  1346.9 15.6 %copy.18 = bf16[2,1152,2304]{2,1,0:T(8,128)(2,1)} copy(bf16[2,1152,2304]{1,2,0:T(8,128)(2,1)} %bitcast.12) | data formatting | bytes 21233664 | tf_op jit(solution)/shard_map/all_to_all | solution.py:39
  1362.5 32.4 %all-reduce.5.cloned.1.call-done = bf16[512,4608]{1,0:T(8,128)(2,1)} async-done(((bf16[512,4608]{1,0:T(8,128)(2,1)}), bf16[512,4608]{1,0:T(8,128)(2,1)}) %all-reduce.5.cloned.1.call-update) | async-done | bytes 4718608 | tf_op jit(solution)/shard_map/psum | solution.py:52
  1400.3 8.3 fusion.32
  1408.6 90.3 %reduce-scatter.5.cloned.1.call-done = f32[32,2304]{1,0:T(8,128)} async-done(((f32[512,2304]{1,0:T(8,128)}), f32[32,2304]{1,0:T(8,128)}) %reduce-scatter.5.cloned.1.call-update) | async-done | bytes 294928 | tf_op jit(solution)/shard_map/reduce_scatter | solution.py:54
  (50 shorter events, 81.6 us)
Async XLA Ops:
  37.6 125.4 %all-to-all-start.2 = ((bf16[1152,2,2304]{0,2,1:T(8,128)(2,1)}), bf16[1152,2,2304]{0,2,1:T(8,128)(2,1)}, u32[]{:S(2)}, u32[]{:S(2)}) async-start(bf16[1152,2,2304]{0,2,1:T(8,128)(2,1)} %bitcast.55), calls=%async_computation.2 | async-start | bytes 21233664 | tf_op jit(solution)/shard_map/all_to_all | solution.py:39
  163.0 195.7 %all-to-all-start = ((bf16[144,2,16,1152]{3,1,0,2:T(2,128)(2,1)}), bf16[144,2,16,1152]{3,1,0,2:T(2,128)(2,1)}, u32[]{:S(2)}, u32[]{:S(2)}) async-start(bf16[144,2,16,1152]{3,1,0,2:T(2,128)(2,1)} %copy.11), calls=%async_computation | async-start | bytes 21233664 | tf_op jit(solution)/shard_map/all_to_all | solution.py:32
  358.7 234.9 %all-to-all-start.1 = ((bf16[144,2,16,1152]{3,1,0,2:T(2,128)(2,1)}), bf16[144,2,16,1152]{3,1,0,2:T(2,128)(2,1)}, u32[]{:S(2)}, u32[]{:S(2)}) async-start(bf16[144,2,16,1152]{3,1,0,2:T(2,128)(2,1)} %copy.12), calls=%async_computation.1 | async-start | bytes 21233664 | tf_op jit(solution)/shard_map/all_to_all | solution.py:33
  427.1 212.0 %copy-start.2 = (bf16[32,2304]{1,0:T(8,128)(2,1)S(1)}, bf16[32,2304]{1,0:T(8,128)(2,1)}, u32[]{:S(2)}) copy-start(bf16[32,2304]{1,0:T(8,128)(2,1)} %param.6) | copy-start | bytes 442372
  427.1 217.1 %copy-start.3 = (f32[2,2304]{1,0:T(2,128)S(1)}, f32[2,2304]{1,0:T(2,128)}, u32[]{:S(2)}) copy-start(f32[2,2304]{1,0:T(2,128)} %param.7) | copy-start | bytes 55300
  593.6 249.1 %all-to-all-start.3 = ((bf16[144,2,16,1152]{3,1,0,2:T(2,128)(2,1)}), bf16[144,2,16,1152]{3,1,0,2:T(2,128)(2,1)}, u32[]{:S(2)}, u32[]{:S(2)}) async-start(bf16[144,2,16,1152]{3,1,0,2:T(2,128)(2,1)} %copy.15), calls=%async_computation.4 | async-start | bytes 21233664 | tf_op jit(solution)/shard_map/all_to_all | solution.py:32
  639.1 249.3 %all-gather.3.cloned.1.call-start = ((), (), s32[]{:S(2)}) async-start(), calls=%async_computation.8 | async-start | bytes 2506752 | tf_op jit(solution)/shard_map/all_gather | solution.py:48
  842.7 328.9 %all-to-all-start.4 = ((bf16[144,2,16,1152]{3,1,0,2:T(2,128)(2,1)}), bf16[144,2,16,1152]{3,1,0,2:T(2,128)(2,1)}, u32[]{:S(2)}, u32[]{:S(2)}) async-start(bf16[144,2,16,1152]{3,1,0,2:T(2,128)(2,1)} %copy.16), calls=%async_computation.5 | async-start | bytes 21233664 | tf_op jit(solution)/shard_map/all_to_all | solution.py:33
  888.1 136.7 %all-reduce.3.cloned.1.call-start = ((), (), s32[]{:S(2)}) async-start(), calls=%async_computation.9 | async-start | bytes 9437184 | tf_op jit(solution)/shard_map/psum | solution.py:52
  905.0 227.0 %reduce-scatter.3.cloned.1.call-start = ((), (), s32[]{:S(2)}) async-start(), calls=%async_computation.10 | async-start | bytes 5013504 | tf_op jit(solution)/shard_map/reduce_scatter | solution.py:54
  1024.8 5.4 copy-start
  1030.2 8.4 copy-start.4
  1038.5 163.4 %all-gather.5.cloned.1.call-start = ((), (), s32[]{:S(2)}) async-start(), calls=%async_computation.11 | async-start | bytes 2506752 | tf_op jit(solution)/shard_map/all_gather | solution.py:48
  1171.6 175.2 %all-to-all-start.5 = ((bf16[1152,2,2304]{0,2,1:T(8,128)(2,1)}), bf16[1152,2,2304]{0,2,1:T(8,128)(2,1)}, u32[]{:S(2)}, u32[]{:S(2)}) async-start(bf16[1152,2,2304]{0,2,1:T(8,128)(2,1)} %bitcast.54), calls=%async_computation.6 | async-start | bytes 21233664 | tf_op jit(solution)/shard_map/all_to_all | solution.py:39
  1179.3 215.6 %all-reduce.5.cloned.1.call-start = ((), (), s32[]{:S(2)}) async-start(), calls=%async_computation.12 | async-start | bytes 9437184 | tf_op jit(solution)/shard_map/psum | solution.py:52
  1218.7 280.3 %reduce-scatter.5.cloned.1.call-start = ((), (), s32[]{:S(2)}) async-start(), calls=%async_computation.13 | async-start | bytes 5013504 | tf_op jit(solution)/shard_map/reduce_scatter | solution.py:54
  1394.9 5.4 copy-start.1
Sparse Core Ops, SparseCore 0:
  645.2 161.6 all-gather.2
  905.2 119.5 all-reduce.2
  1038.7 93.2 reduce-scatter.2
  1145.1 56.8 all-gather.4
  1218.8 176.0 all-reduce.4
  1408.7 90.1 reduce-scatter.4
where the time goes:
time: 1520 us; the launch traced here: 1510 us
  waiting for transfers between devices  1020 us (67%)
  local copies, waits for them, and re-layouts  237 us (16%)
  starting transfers between devices  159 us (10%)
  matrix products  49.9 us (3%)
  blocking collectives  19.7 us (1%)
    all_to_all x2, waiting for transfers between devices, on_device(): lax.all_to_all(gate_split, 'col', split_axis=2, concat_axis=0, tiled=True)  309 us
    all_to_all x2, waiting for transfers between devices, on_device(): lax.all_to_all(down_weight[layer_index], 'row', split_axis=1, concat_axis...  214 us
    reduce_scatter x2, waiting for transfers between devices, on_device(): lax.psum_scatter(jnp.dot(hidden, down_tile, preferred_element_type=jnp.fl...  184 us
    all_to_all x2, waiting for transfers between devices, on_device(): lax.all_to_all(up_split, 'col', split_axis=2, concat_axis=0, tiled=True)  166 us
    psum x2, waiting for transfers between devices, on_device(): lax.psum(partial_sums.astype(jnp.bfloat16), 'row').astype(jnp.float32)  136 us
    unnamed x20, local copies, waits for them, and re-layouts  101 us
    all_to_all x2, starting transfers between devices, on_device(): lax.all_to_all(up_split, 'col', split_axis=2, concat_axis=0, tiled=True)  90.9 us
    all_to_all x2, starting transfers between devices, on_device(): lax.all_to_all(gate_split, 'col', split_axis=2, concat_axis=0, tiled=True)  51.8 us
  transfers between devices with their start and end apart: 12, of which 10 were waited for; matrix products, arithmetic and copies ran while one was open for 17% of the time, Pallas kernels for 0%

commit v1 on v0

--- a/solution.py
+++ b/solution.py
@@ -1,9 +1,19 @@
+import functools
 import jax
 import jax.numpy as jnp
 from jax import lax
 from jax.sharding import PartitionSpec as P
 
 norm_eps = 1e-06
+
+
+def _push_ratios(state, named_axis):
+    part_now = lax.all_gather(state, named_axis)
+    fresh = jnp.sum(part_now, axis=0)
+    return fresh
+
+
+attach_racks = functools.partial(_push_ratios, named_axis="row")
 
 
 def activate(summed, columns):
@@ -49,7 +59,7 @@
             gate_up,
             preferred_element_type=jnp.float32,
         )
-        summed = lax.psum(partial_sums.astype(jnp.bfloat16), "row").astype(jnp.float32)
+        summed = attach_racks(partial_sums.astype(jnp.bfloat16)).astype(jnp.float32)
         hidden = activate(summed, columns)
         branch = lax.psum_scatter(
             jnp.dot(hidden, down_tile, preferred_element_type=jnp.float32),

time: 1520 us -> 1570 us (1.033)
  blocking collectives: 19.7 us -> 234 us
  waiting for transfers between devices: 1020 us -> 848 us
  other arithmetic: 14.3 us -> 32.1 us
    all_to_all x0 -> x1, blocking collectives: none -> 215 us  [on_device(): lax.all_to_all(down_weight[layer_index], 'row', split_axis=1, concat_axis...]
    all_gather x2, waiting for transfers between devices: 11 us -> 176 us  [on_device(): lax.all_gather(normed, 'col', axis=0, tiled=True)]
    all_to_all x2, waiting for transfers between devices: 309 us -> 157 us  [on_device(): lax.all_to_all(gate_split, 'col', split_axis=2, concat_axis=0, tiled=True)]
    psum x2 -> x0, waiting for transfers between devices: 136 us -> none  [on_device(): lax.psum(partial_sums.astype(jnp.bfloat16), 'row').astype(jnp.float32)]
    all_to_all x2 -> x1, waiting for transfers between devices: 214 us -> 85.5 us  [on_device(): lax.all_to_all(down_weight[layer_index], 'row', split_axis=1, concat_axis...]
    all_gather x0 -> x2, waiting for transfers between devices: none -> 59.7 us  [_push_ratios(): part_now = lax.all_gather(state, named_axis)]
    reduce_scatter x2, waiting for transfers between devices: 184 us -> 203 us  [on_device(): lax.psum_scatter(jnp.dot(hidden, down_tile, preferred_element_type=jnp.fl...]
    reduce_sum x0 -> x2, other arithmetic: none -> 17.8 us  [_push_ratios(): fresh = jnp.sum(part_now, axis=0)]
  transfers between devices with their start and end apart: 12 -> 11, of which waited for: 10 -> 8; matrix products, arithmetic and copies ran while one was open for 17% -> 16% of each run, Pallas kernels for 0% -> 0%
where the time goes in v1:
time: 1570 us; the launch traced here: 1560 us
  waiting for transfers between devices  848 us (54%)
  local copies, waits for them, and re-layouts  237 us (15%)
  blocking collectives  234 us (15%)
  starting transfers between devices  148 us (9%)
  matrix products  49.8 us (3%)
  other arithmetic  32.1 us (2%)
    all_to_all x1, blocking collectives, on_device(): lax.all_to_all(down_weight[layer_index], 'row', split_axis=1, concat_axis...  215 us
    reduce_scatter x2, waiting for transfers between devices, on_device(): lax.psum_scatter(jnp.dot(hidden, down_tile, preferred_element_type=jnp.fl...  203 us
    all_gather x2, waiting for transfers between devices, on_device(): lax.all_gather(normed, 'col', axis=0, tiled=True)  176 us
    all_to_all x2, waiting for transfers between devices, on_device(): lax.all_to_all(up_split, 'col', split_axis=2, concat_axis=0, tiled=True)  166 us
    all_to_all x2, waiting for transfers between devices, on_device(): lax.all_to_all(gate_split, 'col', split_axis=2, concat_axis=0, tiled=True)  157 us
    unnamed x20, local copies, waits for them, and re-layouts  101 us
    all_to_all x2, starting transfers between devices, on_device(): lax.all_to_all(up_split, 'col', split_axis=2, concat_axis=0, tiled=True)  87.1 us
    all_to_all x1, waiting for transfers between devices, on_device(): lax.all_to_all(down_weight[layer_index], 'row', split_axis=1, concat_axis...  85.5 us
  transfers between devices with their start and end apart: 11, of which 8 were waited for; matrix products, arithmetic and copies ran while one was open for 16% of the time, Pallas kernels for 0%

profile of v1, /device:TPU:0, one launch (start us, length us, event | category | flops | bytes accessed | tf_op | source)
XLA Modules:
  0.0 1562.1 jit_solution(11301309608102874984)
XLA Ops:
  6.5 15.8 %fusion.65 = (bf16[1,1152,4608]{2,1,0:T(8,128)(2,1)}, bf16[1,1152,4608]{2,1,0:T(8,128)(2,1)}) fusion(bf16[2,1152,4608]{2,1,0:T(8,128)(2,1)} %param.11), kind=kLoop, calls=%fused_computation.76 | loop fusion | bytes 42467328 | tf_op jit(solution)/shard_map/slice | solution.py:50
  22.3 15.2 copy.19
  45.4 12.6 fusion.63
  61.7 15.8 %copy.11 = bf16[144,2,16,1152]{3,1,0,2:T(2,128)(2,1)} copy(bf16[144,2,16,1152]{3,2,1,0:T(8,128)(2,1)S(1)} %bitcast.57) | data formatting | bytes 21233664 | tf_op jit(solution)/shard_map/reshape;squeeze | solution.py:37
  77.5 85.5 %all-to-all-done.2 = bf16[1152,2,2304]{0,2,1:T(8,128)(2,1)} async-done(((bf16[1152,2,2304]{0,2,1:T(8,128)(2,1)}), bf16[1152,2,2304]{0,2,1:T(8,128)(2,1)}, u32[]{:S(2)}, u32[]{:S(2)}) %all-to-all-start.2) | async-done | bytes 10616864 | tf_op jit(solution)/shard_map/all_to_all | solution.py:49
  169.3 12.6 fusion.64
  185.5 15.8 %copy.12 = bf16[144,2,16,1152]{3,1,0,2:T(2,128)(2,1)} copy(bf16[144,2,16,1152]{3,2,1,0:T(8,128)(2,1)S(1)} %bitcast.58) | data formatting | bytes 21233664 | tf_op jit(solution)/shard_map/reshape;squeeze | solution.py:40
  201.4 157.3 %all-to-all-done = bf16[144,2,16,1152]{3,1,0,2:T(2,128)(2,1)} async-done(((bf16[144,2,16,1152]{3,1,0,2:T(2,128)(2,1)}), bf16[144,2,16,1152]{3,1,0,2:T(2,128)(2,1)}, u32[]{:S(2)}, u32[]{:S(2)}) %all-to-all-start) | async-done | bytes 10616864 | tf_op jit(solution)/shard_map/all_to_all | solution.py:42
  358.7 45.5 %all-to-all-start.1 = ((bf16[144,2,16,1152]{3,1,0,2:T(2,128)(2,1)}), bf16[144,2,16,1152]{3,1,0,2:T(2,128)(2,1)}, u32[]{:S(2)}, u32[]{:S(2)}) async-start(bf16[144,2,16,1152]{3,1,0,2:T(2,128)(2,1)} %copy.12), calls=%async_computation.1 | async-start | bytes 21233664 | tf_op jit(solution)/shard_map/all_to_all | solution.py:43
  411.3 15.8 %copy.15 = bf16[144,2,16,1152]{3,1,0,2:T(2,128)(2,1)} copy(bf16[144,2,16,1152]{3,2,1,0:T(8,128)(2,1)S(1)} %bitcast.59) | data formatting | bytes 21233664 | tf_op jit(solution)/shard_map/reshape;squeeze | solution.py:37
  427.2 166.4 %all-to-all-done.1 = bf16[144,2,16,1152]{3,1,0,2:T(2,128)(2,1)} async-done(((bf16[144,2,16,1152]{3,1,0,2:T(2,128)(2,1)}), bf16[144,2,16,1152]{3,1,0,2:T(2,128)(2,1)}, u32[]{:S(2)}, u32[]{:S(2)}) %all-to-all-start.1) | async-done | bytes 10616864 | tf_op jit(solution)/shard_map/all_to_all | solution.py:43
  593.6 45.5 %all-to-all-start.3 = ((bf16[144,2,16,1152]{3,1,0,2:T(2,128)(2,1)}), bf16[144,2,16,1152]{3,1,0,2:T(2,128)(2,1)}, u32[]{:S(2)}, u32[]{:S(2)}) async-start(bf16[144,2,16,1152]{3,1,0,2:T(2,128)(2,1)} %copy.15), calls=%async_computation.4 | async-start | bytes 21233664 | tf_op jit(solution)/shard_map/all_to_all | solution.py:42
  645.3 11.4 copy.22
  656.7 11.3 copy.24
  668.0 138.9 %all-gather.7.cloned.1.call-done = bf16[512,2304]{1,0:T(8,128)(2,1)} async-done(((bf16[32,2304]{1,0:T(8,128)(2,1)}), bf16[512,2304]{1,0:T(8,128)(2,1)}) %all-gather.7.cloned.1.call-update) | async-done | bytes 2359312 | tf_op jit(solution)/shard_map/all_gather | solution.py:58
  806.9 16.6 %fusion.11 = bf16[512,4608]{1,0:T(8,128)(2,1)} fusion(bf16[512,2304]{1,0:T(8,128)(2,1)} %all-gather.7.cloned.1.call-done, bf16[2304,2304]{1,0:T(8,128)(2,1)} %bitcast.71, bf16[2304,2304]{1,0:T(8,128)(2,1)} %bitcast.70), kind=kOutput, calls=%fused_computation.9 | convolution fusion | flops 10916462592 | bytes 28311552 | tf_op jit(solution)/shard_map/dot_general | solution.py:57
  830.6 15.9 %copy.16 = bf16[144,2,16,1152]{3,1,0,2:T(2,128)(2,1)} copy(bf16[144,2,16,1152]{3,2,1,0:T(8,128)(2,1)S(1)} %bitcast.60) | data formatting | bytes 21233664 | tf_op jit(solution)/shard_map/reshape;squeeze | solution.py:40
  846.5 41.6 %all-to-all-start.4 = ((bf16[144,2,16,1152]{3,1,0,2:T(2,128)(2,1)}), bf16[144,2,16,1152]{3,1,0,2:T(2,128)(2,1)}, u32[]{:S(2)}, u32[]{:S(2)}) async-start(bf16[144,2,16,1152]{3,1,0,2:T(2,128)(2,1)} %copy.16), calls=%async_computation.5 | async-start | bytes 21233664 | tf_op jit(solution)/shard_map/all_to_all | solution.py:43
  888.4 15.6 copy.14
  904.0 59.7 %all-gather.11.cloned.1.call-done = bf16[1024,4608]{1,0:T(8,128)(2,1)} async-done(((bf16[512,4608]{1,0:T(8,128)(2,1)}), bf16[1024,4608]{1,0:T(8,128)(2,1)}) %all-gather.11.cloned.1.call-update) | async-done | bytes 9437200 | tf_op jit(solution)/shard_map/all_gather | solution.py:11
  963.7 8.8 reduce_sum.61
  978.0 8.3 fusion.34
  986.4 126.9 %reduce-scatter.3.cloned.1.call-done = f32[32,2304]{1,0:T(8,128)} async-done(((f32[512,2304]{1,0:T(8,128)}), f32[32,2304]{1,0:T(8,128)}) %reduce-scatter.3.cloned.1.call-update) | async-done | bytes 294928 | tf_op jit(solution)/shard_map/reduce_scatter | solution.py:64
  1126.5 11.4 copy.26
  1137.9 11.3 copy.28
  1149.2 37.2 %all-gather.9.cloned.1.call-done = bf16[512,2304]{1,0:T(8,128)(2,1)} async-done(((bf16[32,2304]{1,0:T(8,128)(2,1)}), bf16[512,2304]{1,0:T(8,128)(2,1)}) %all-gather.9.cloned.1.call-update) | async-done | bytes 2359312 | tf_op jit(solution)/shard_map/all_gather | solution.py:58
  1186.5 16.6 %fusion.8 = bf16[512,4608]{1,0:T(8,128)(2,1)} fusion(bf16[512,2304]{1,0:T(8,128)(2,1)} %all-gather.9.cloned.1.call-done, bf16[2304,2304]{1,0:T(8,128)(2,1)} %bitcast.72, bf16[2304,2304]{1,0:T(8,128)(2,1)} %bitcast.67), kind=kOutput, calls=%fused_computation.8 | convolution fusion | flops 10916462592 | bytes 28311552 | tf_op jit(solution)/shard_map/dot_general | solution.py:57
  1203.2 15.7 %copy.20 = bf16[1,1152,4608]{1,2,0:T(8,128)(2,1)} copy(bf16[1,1152,4608]{2,1,0:T(8,128)(2,1)} %get-tuple-element.15) | data formatting | bytes 21233664
  1218.9 214.7 %all_to_all.98 = bf16[1152,2,2304]{0,2,1:T(8,128)(2,1)} all-to-all(bf16[1152,2,2304]{0,2,1:T(8,128)(2,1)} %bitcast.61), channel_id=1, replica_groups=mesh['row'=2,'col'=16] {'row'}, dimensions={1} | all-to-all | bytes 21233664 | tf_op jit(solution)/shard_map/all_to_all | solution.py:49
  1433.6 15.5 copy.18
  1449.1 8.9 reduce_sum.64
  1471.8 75.7 %reduce-scatter.5.cloned.1.call-done = f32[32,2304]{1,0:T(8,128)} async-done(((f32[512,2304]{1,0:T(8,128)}), f32[32,2304]{1,0:T(8,128)}) %reduce-scatter.5.cloned.1.call-update) | async-done | bytes 294928 | tf_op jit(solution)/shard_map/reduce_scatter | solution.py:64
  (51 shorter events, 82.5 us)
Async XLA Ops:
  37.6 125.4 %all-to-all-start.2 = ((bf16[1152,2,2304]{0,2,1:T(8,128)(2,1)}), bf16[1152,2,2304]{0,2,1:T(8,128)(2,1)}, u32[]{:S(2)}, u32[]{:S(2)}) async-start(bf16[1152,2,2304]{0,2,1:T(8,128)(2,1)} %bitcast.56), calls=%async_computation.2 | async-start | bytes 21233664 | tf_op jit(solution)/shard_map/all_to_all | solution.py:49
  163.0 195.7 %all-to-all-start = ((bf16[144,2,16,1152]{3,1,0,2:T(2,128)(2,1)}), bf16[144,2,16,1152]{3,1,0,2:T(2,128)(2,1)}, u32[]{:S(2)}, u32[]{:S(2)}) async-start(bf16[144,2,16,1152]{3,1,0,2:T(2,128)(2,1)} %copy.11), calls=%async_computation | async-start | bytes 21233664 | tf_op jit(solution)/shard_map/all_to_all | solution.py:42
  358.7 234.9 %all-to-all-start.1 = ((bf16[144,2,16,1152]{3,1,0,2:T(2,128)(2,1)}), bf16[144,2,16,1152]{3,1,0,2:T(2,128)(2,1)}, u32[]{:S(2)}, u32[]{:S(2)}) async-start(bf16[144,2,16,1152]{3,1,0,2:T(2,128)(2,1)} %copy.12), calls=%async_computation.1 | async-start | bytes 21233664 | tf_op jit(solution)/shard_map/all_to_all | solution.py:43
  427.2 212.0 %copy-start.2 = (bf16[32,2304]{1,0:T(8,128)(2,1)S(1)}, bf16[32,2304]{1,0:T(8,128)(2,1)}, u32[]{:S(2)}) copy-start(bf16[32,2304]{1,0:T(8,128)(2,1)} %param.6) | copy-start | bytes 442372
  427.2 217.0 %copy-start.3 = (f32[2,2304]{1,0:T(2,128)S(1)}, f32[2,2304]{1,0:T(2,128)}, u32[]{:S(2)}) copy-start(f32[2,2304]{1,0:T(2,128)} %param.7) | copy-start | bytes 55300
  593.6 252.9 %all-to-all-start.3 = ((bf16[144,2,16,1152]{3,1,0,2:T(2,128)(2,1)}), bf16[144,2,16,1152]{3,1,0,2:T(2,128)(2,1)}, u32[]{:S(2)}, u32[]{:S(2)}) async-start(bf16[144,2,16,1152]{3,1,0,2:T(2,128)(2,1)} %copy.15), calls=%async_computation.4 | async-start | bytes 21233664 | tf_op jit(solution)/shard_map/all_to_all | solution.py:42
  639.1 167.8 %all-gather.7.cloned.1.call-start = ((), (), s32[]{:S(2)}) async-start(), calls=%async_computation.8 | async-start | bytes 2506752 | tf_op jit(solution)/shard_map/all_gather | solution.py:58
  645.1 318.6 %all-gather.11.cloned.1.call-start = ((), (), s32[]{:S(2)}) async-start(), calls=%async_computation.12 | async-start | bytes 14155776 | tf_op jit(solution)/shard_map/all_gather | solution.py:11
  846.5 291.4 %all-to-all-start.4 = ((bf16[144,2,16,1152]{3,1,0,2:T(2,128)(2,1)}), bf16[144,2,16,1152]{3,1,0,2:T(2,128)(2,1)}, u32[]{:S(2)}, u32[]{:S(2)}) async-start(bf16[144,2,16,1152]{3,1,0,2:T(2,128)(2,1)} %copy.16), calls=%async_computation.5 | async-start | bytes 21233664 | tf_op jit(solution)/shard_map/all_to_all | solution.py:43
  888.1 225.1 %reduce-scatter.3.cloned.1.call-start = ((), (), s32[]{:S(2)}) async-start(), calls=%async_computation.9 | async-start | bytes 5013504 | tf_op jit(solution)/shard_map/reduce_scatter | solution.py:64
  972.5 5.4 copy-start.1
  977.9 8.4 copy-start.4
  986.3 200.2 %all-gather.9.cloned.1.call-start = ((), (), s32[]{:S(2)}) async-start(), calls=%async_computation.10 | async-start | bytes 2506752 | tf_op jit(solution)/shard_map/all_gather | solution.py:58
  1126.2 322.9 %all-gather.13.cloned.1.call-start = ((), (), s32[]{:S(2)}) async-start(), calls=%async_computation.13 | async-start | bytes 14155776 | tf_op jit(solution)/shard_map/all_gather | solution.py:11
  1203.1 344.4 %reduce-scatter.5.cloned.1.call-start = ((), (), s32[]{:S(2)}) async-start(), calls=%async_computation.11 | async-start | bytes 5013504 | tf_op jit(solution)/shard_map/reduce_scatter | solution.py:64
  1458.0 5.4 copy-start
Sparse Core Ops, SparseCore 0:
  645.2 161.6 all-gather.6
  823.6 139.9 all-gather.10
  986.4 126.8 reduce-scatter.2
  1126.3 60.0 all-gather.8
  1203.3 201.5 all-gather.12
  1471.9 75.5 reduce-scatter.4
